TPU v7x, 8 devices: a whole 2x2x1 slice. The times are simulated.
8 devices in a mesh: pairs: 2 (over z, y), rows: 4 (over x, core).
Axes of the slice: x: 2, y: 2, z: 1, core: 2. Of those that a mesh axis runs over, the one named last changes fastest.
Arguments:
- cost_src: float32 [4096, 2048], P(('pairs', 'rows')), parts along dimension 0
- cost_tgt: float32 [2048, 1024], P(('pairs', 'rows')), parts along dimension 0
- plan_init: float32 [4096, 1024], P(('pairs', 'rows')), parts along dimension 0
- mass_src: float32 [4096], P(('pairs', 'rows')), parts along dimension 0
- mass_tgt: float32 [2048], P('pairs'), parts along dimension 0
- feat_src: float32 [4096, 256], P(('pairs', 'rows')), parts along dimension 0
- feat_tgt: float32 [2048, 256], P(('pairs', 'rows')), parts along dimension 0
- epsilon: float32 [], replicated
Outputs:
- output: float32 [4096, 1024], P(('pairs', 'rows')), parts along dimension 0
There are 2 independent parts. A program takes and returns all parts, laid end to end along the dimension named above; an argument that names none is the same for every part.
All inputs are finite; a program needn't handle non-finite values.
Results may differ from a plain program's by a relative error of at most 0.001.
Values are sent between devices in bfloat16 or wider.
A program may use at most 1 GiB of HBM per device.

v0:
```python
import jax
import jax.numpy as jnp
from jax import lax
from jax.experimental import pallas as pl
from jax.experimental.pallas import tpu as pltpu
from jax.sharding import PartitionSpec as P

ALPHA = 0.5
OUTER_STEPS = 2
SWEEPS = 10
LOG2E = 1.4426950408889634

N = 2048
M = 1024
D = 256
NB = 512
MB = 256
F32 = jnp.float32
BF16 = jnp.bfloat16
LANES = 128
COLS = M // LANES

T_CHUNKS = 4
TR = NB // T_CHUNKS
CH = 256
HALF = NB // 2
FORM_GROUP = 32


class Slots:
    def __init__(self):
        self.names = {}

    def __call__(self, name):
        return self.names.setdefault(name, len(self.names))


LINK = Slots()
SIDE = Slots()
for k in range(T_CHUNKS):
    LINK(("t", k)), SIDE(("t", k)), SIDE(("far t", k))
for k in range(4):
    LINK(("c2", k)), SIDE(("far c2", k)), LINK(("c1 strip", k))
for k in range(4):
    SIDE(("a1", k))
for k in range(2):
    SIDE(("a2", k))
for k in range(2):
    LINK(("c1 quad", k)), SIDE(("c1 quad", k))
for k in range(2):
    LINK(("x", k)), SIDE(("far x", k))
for name in ("y", "p"):
    LINK(name), SIDE(name), SIDE("far " + name)
SIDE("c2"), SIDE("c1"), SIDE("x")


def hint(value, multiple):
    return value if isinstance(value, int) else pl.multiple_of(value, multiple)


def span(start, size):
    return pl.ds(hint(start, size), size)


def col(j):
    return slice(j * LANES, (j + 1) * LANES)


def tree(op, parts):
    while len(parts) > 1:
        parts = [op(parts[i], parts[i + 1]) for i in range(0, len(parts), 2)]
    return parts[0]


def store_col_scale(acc, v_ref, q_ref):
    for j in range(COLS):
        col_sum = jnp.sum(acc[j], axis=0, keepdims=True)
        v_ref[:, col(j)] = jnp.broadcast_to(q_ref[:, col(j)] / col_sum, (8, LANES))


def sweeps(count, kern, plan_b, u_b, v_ref, q_ref, group):
    lead = 128
    shape = (group // 8, 8, LANES)

    def sweep(_, carry):
        v = [v_ref[:, col(j)][None] for j in range(COLS)]

        def tile(row, j):
            return kern[row:row + group, col(j)].reshape(shape)

        acc = [jnp.zeros((8, LANES), F32) for _ in range(COLS)]
        for row in range(-lead, N, group):
            top = row + lead
            if top < N:
                total = tree(jnp.add, [tile(top, j) * v[j] for j in range(COLS)])
                u = plan_b[top:top + group, :].reshape(shape) / jnp.sum(total, axis=2, keepdims=True)
                u_b[top:top + group, :] = u.reshape(group, LANES)
            if row >= 0:
                u = u_b[row:row + group, :].reshape(shape)
                acc = [acc[j] + jnp.sum(tile(row, j) * u, axis=0) for j in range(COLS)]
        store_col_scale(acc, v_ref, q_ref)
        return carry

    lax.fori_loop(0, count, sweep, 0)


def scaled_rows(kern, u_b, v_ref, row, count):
    u = u_b[pl.ds(row, count), :].reshape(count // 8, 8, LANES)
    for j in range(COLS):
        k = kern[pl.ds(row, count), col(j)].reshape(count // 8, 8, LANES)
        yield j, (u * k * v_ref[:, col(j)][None]).reshape(count, LANES)


def kernel(c1_hbm, c2_hbm, t0_hbm, p_hbm, q_hbm, x_hbm, y_hbm, eps_ref, out_ref,
           q_ref, t_st, t_all, c1_rows, c1_side, quad_side, c2_all, y_all, x_all, g_all, a1_all, a2_all,
           kern, p_all, p_b, u_b, peak_b, first_b, acc_ref, v_ref,
           load_sem, link_send, link_recv, side_send, side_recv):
    raw0, raw1 = 0, CH
    me = lax.axis_index("rows")
    chip = me // 2
    core = me % 2
    partner = chip * 2 + (1 - core)
    far = (1 - chip) * 2 + core
    far_partner = (1 - chip) * 2 + (1 - core)

    y_st, x_st, c2_st = kern.at[:MB, :D], kern.at[MB:MB + NB, :D], kern.at[MB + NB:2 * MB + NB, :]
    loads = {}
    for i, (name, src, dst) in enumerate((
            ("y", y_hbm, y_st), ("p", p_hbm, p_all.at[me]), ("t", t0_hbm, t_st), ("c2", c2_hbm, c2_st), ("x", x_hbm, x_st),
            ("left", c1_hbm.at[:, :M], g_all.at[:NB]), ("right", c1_hbm.at[:, M:], g_all.at[NB:2 * NB]), ("q", q_hbm, q_ref))):
        loads[name] = pltpu.make_async_copy(src, dst, load_sem.at[i])
        loads[name].start()

    barrier = pltpu.get_barrier_semaphore()
    for peer in (partner, far):
        pl.semaphore_signal(barrier, inc=1, device_id={"rows": peer}, device_id_type=pl.DeviceIdType.MESH)
    pl.semaphore_wait(barrier, 2)

    def to_far(src, dst, name):
        slot = LINK.names[name]
        return pltpu.make_async_remote_copy(
            src_ref=src, dst_ref=dst, send_sem=link_send.at[slot], recv_sem=link_recv.at[slot],
            device_id={"rows": far}, device_id_type=pl.DeviceIdType.MESH)

    def to_partner(src, dst, name):
        slot = SIDE.names[name]
        return pltpu.make_async_remote_copy(
            src_ref=src, dst_ref=dst, send_sem=side_send.at[slot], recv_sem=side_recv.at[slot],
            device_id={"rows": partner}, device_id_type=pl.DeviceIdType.MESH)

    sends = []

    def go(copy):
        copy.start()
        sends.append(copy)

    def far_arrived(ref, name):
        to_far(ref, ref, name).wait_recv()

    def partner_arrived(ref, name):
        to_partner(ref, ref, name).wait_recv()

    def t_rows(owner, k):
        return t_all.at[span(owner * NB + k * TR, TR), :]

    def c2_rows(owner):
        return c2_all.at[span(owner * MB, MB), :]

    def c2_pieces(owner, other, which):
        return (
            c2_all.at[span(owner * MB + 128, 128), span(other * MB, 128)],
            c2_all.at[span(owner * MB + which * 128, 128), span(other * MB + which * 128, 128)],
            c2_all.at[span(owner * MB, 128), span(owner * MB, MB)],
            c2_all.at[span(owner * MB + 128, 128), span(owner * MB + 128, 128)])

    def y_rows(owner):
        return y_all.at[span(owner * MB, MB), :]

    def x_rows(owner):
        return x_all.at[span(owner * NB, NB), :]

    def x_half(owner, k):
        return x_all.at[span(owner * NB + k * CH, CH), :]

    def c1_quads(base, other, which):
        return (c1_rows.at[base + HALF:base + NB, span(other * NB, HALF)],
                c1_rows.at[span(base + which * HALF, HALF), span(other * NB + which * HALF, HALF)])

    def c1_strip(base, owner, k):
        return c1_rows.at[base + k * 128:base + (k + 1) * 128, pl.ds(hint(owner * NB + k * 128, 128), NB - k * 128)]

    loads["y"].wait()
    y_all[span(me * MB, MB), :] = kern[:MB, :D].astype(BF16)
    loads["p"].wait()
    go(to_far(p_all.at[me], p_all.at[me], "p"))
    go(to_partner(p_all.at[me], p_all.at[me], "p"))
    go(to_far(y_rows(me), y_rows(me), "y"))
    go(to_partner(y_rows(me), y_rows(me), "y"))
    loads["t"].wait()
    for k in range(T_CHUNKS):
        t_all[span(me * NB + k * TR, TR), :] = t_st[k * TR:(k + 1) * TR, :].astype(BF16)
    for k in range(T_CHUNKS):
        go(to_far(t_rows(me, k), t_rows(me, k), ("t", k)))
    for k in range(T_CHUNKS):
        go(to_partner(t_rows(me, k), t_rows(me, k), ("t", k)))
    for name in ("c2", "x", "left", "right", "q"):
        loads[name].wait()
    c2_all[span(me * MB, MB), :] = kern[MB + NB:2 * MB + NB, :].astype(BF16)
    x_all[span(me * NB, NB), :] = kern[MB:MB + NB, :D].astype(BF16)
    c1_rows[:NB, :M] = g_all[:NB, :].astype(BF16)
    c1_rows[:NB, M:] = g_all[NB:2 * NB, :].astype(BF16)
    for k, piece in enumerate(c2_pieces(me, partner, core)):
        go(to_far(piece, piece, ("c2", k)))
    for k, (src, dst) in enumerate(zip(c1_quads(0, partner, core), c1_quads(NB, partner, core))):
        go(to_far(src, dst, ("c1 quad", k)))
    for k in range(4):
        go(to_far(c1_strip(0, me, k), c1_strip(NB, me, k), ("c1 strip", k)))
    for k in range(2):
        go(to_far(x_half(me, k), x_half(me, k), ("x", k)))
    go(to_partner(c2_rows(me), c2_rows(me), "c2"))
    go(to_partner(x_rows(me), x_rows(me), "x"))
    go(to_partner(c1_rows.at[:NB, span(far_partner * NB, NB)], c1_side, "c1"))

    def mirror(src, src_row, src_col, dst, dst_row, dst_col, size):
        for i in range(size // LANES):
            for j in range(size // LANES):
                tile = src[span(src_row + i * LANES, LANES), span(src_col + j * LANES, LANES)]
                dst[span(dst_row + j * LANES, LANES), span(dst_col + i * LANES, LANES)] = (
                    tile.astype(F32).T.astype(BF16))

    mirror(c1_rows, 0, far * NB, c1_rows, NB, me * NB, NB)
    partner_arrived(c1_side, "c1")
    mirror(c1_side, 0, 0, c1_rows, NB, partner * NB, NB)
    partner_arrived(c2_rows(partner), "c2")
    mirror(c2_all, chip * 2 * MB, (1 - chip) * 2 * MB, c2_all, (1 - chip) * 2 * MB, chip * 2 * MB, 2 * MB)
    partner_arrived(y_rows(partner), "y")
    partner_arrived(p_all.at[partner], "p")
    partner_arrived(x_rows(partner), "x")

    def forward(ref, name):
        far_arrived(ref, name)
        go(to_partner(ref, ref, ("far " + name[0], name[1]) if isinstance(name, tuple) else "far " + name))

    def gram(owner):
        for n in range(4):
            g = lax.dot_general(x_all[span(owner * NB, NB), :], y_all[n * 256:(n + 1) * 256, :],
                                (((1,), (1,)), ((), ())), preferred_element_type=F32)
            g_all[span(owner * NB, NB), n * 256:(n + 1) * 256] = (2.0 * ALPHA) * g

    def grams(first, second):
        def one(i, carry):
            gram(first + i * (second - first))
            return carry
        lax.fori_loop(0, 2, one, 0)

    forward(y_rows(far), "y")
    forward(p_all.at[far], "p")
    partner_arrived(y_rows(far_partner), "far y")
    partner_arrived(p_all.at[far_partner], "far p")
    for owner in range(4):
        for i in range(NB // LANES):
            block = jnp.broadcast_to(p_all[owner, i:i + 1, :], (LANES, LANES))
            p_b[owner * NB + i * LANES:owner * NB + (i + 1) * LANES, :] = block.T
    grams(me, partner)
    for k in range(T_CHUNKS):
        partner_arrived(t_rows(partner, k), ("t", k))
    for k in range(T_CHUNKS):
        forward(t_rows(far, k), ("t", k))
    for k in range(T_CHUNKS):
        partner_arrived(t_rows(far_partner, k), ("far t", k))

    scale = LOG2E / eps_ref[0, 0]

    def a_rows(a_all, local, base, rows=CH):
        for n in range(4):
            a_all[span(base, rows), n * 256:(n + 1) * 256] = jnp.dot(
                c1_rows[span(local, rows), :], t_all[:, n * 256:(n + 1) * 256], preferred_element_type=F32).astype(BF16)

    def scores(a_all, base, raw):
        for n in range(4):
            b = jnp.dot(a_all[span(base, CH), :], c2_all[:, n * 256:(n + 1) * 256], preferred_element_type=F32)
            t_st[raw:raw + CH, n * 256:(n + 1) * 256] = g_all[span(base, CH), n * 256:(n + 1) * 256] + (2.0 * (1.0 - ALPHA)) * b

    def products(a_all, base):
        for n in range(4):
            b = jnp.dot(a_all[span(base, CH), :], c2_all[:, n * 256:(n + 1) * 256], preferred_element_type=F32)
            g_all[span(base, CH), n * 256:(n + 1) * 256] = (2.0 * (1.0 - ALPHA)) * b

    def late_scores(base, raw):
        for n in range(4):
            g = (2.0 * ALPHA) * lax.dot_general(x_all[span(base, CH), :], y_all[n * 256:(n + 1) * 256, :],
                                                (((1,), (1,)), ((), ())), preferred_element_type=F32)
            t_st[raw:raw + CH, n * 256:(n + 1) * 256] = g + g_all[span(base, CH), n * 256:(n + 1) * 256]
            g_all[span(base, CH), n * 256:(n + 1) * 256] = g

    def form(base, raw):
        acc = [acc_ref[:, col(j)] for j in range(COLS)]
        lead = 64
        group = FORM_GROUP
        shape = (group // 8, 8, LANES)
        for row in range(-2 * lead, CH, group):
            top = row + 2 * lead
            if top < CH:
                peak = tree(jnp.maximum, [t_st[raw + top:raw + top + group, col(j)] for j in range(COLS)])
                peak_b[raw + top:raw + top + group, :] = jnp.broadcast_to(jnp.max(peak, axis=1, keepdims=True), (group, LANES))
            mid = row + lead
            if 0 <= mid < CH:
                here = pl.ds(hint(base + mid, group), group)
                peak = peak_b[raw + mid:raw + mid + group, :]
                vals = [jnp.exp2((t_st[raw + mid:raw + mid + group, col(j)] - peak) * scale) for j in range(COLS)]
                for j in range(COLS):
                    kern[here, col(j)] = vals[j]
                    t_st[raw + mid:raw + mid + group, col(j)] = vals[j]
                total = jnp.sum(tree(jnp.add, vals), axis=1, keepdims=True)
                first_b[raw + mid:raw + mid + group, :] = p_b[here, :] / total
            if row >= 0:
                u = first_b[raw + row:raw + row + group, :].reshape(shape)
                acc = [acc[j] + jnp.sum(t_st[raw + row:raw + row + group, col(j)].reshape(shape) * u, axis=0)
                       for j in range(COLS)]
        for j in range(COLS):
            acc_ref[:, col(j)] = acc[j]

    def b_rows(a_all, bases, ready=None):
        raws = (raw0, raw1)
        for i, base in enumerate(bases):
            if ready and ready[i]:
                ready[i]()
            scores(a_all, base, raws[i % 2])
            if i:
                form(bases[i - 1], raws[(i - 1) % 2])
        form(bases[-1], raws[(len(bases) - 1) % 2])

    def a_slice(a_all, base):
        return a_all.at[span(base, CH), :]

    def my_base(i):
        return jnp.where(i < 2, me * NB + i * CH, far * NB + (i - 2) * CH)

    def their_base(i):
        return jnp.where(i < 2, partner * NB + i * CH, far_partner * NB + (i - 2) * CH)

    mine = [my_base(i) for i in range(4)]
    theirs = [their_base(i) for i in range(4)]

    def share(a_all, name, start, stop):
        slot = SIDE.names[(name, 0)]

        def piece(i):
            ref = a_slice(a_all, my_base(i))
            return pltpu.make_async_remote_copy(
                src_ref=ref, dst_ref=ref, send_sem=side_send.at[slot + i], recv_sem=side_recv.at[slot + i],
                device_id={"rows": partner}, device_id_type=pl.DeviceIdType.MESH)

        def step(i, carry):
            a_rows(a_all, i * CH, my_base(i))
            piece(i).start()
            return carry
        if stop - start == 1:
            step(start, 0)
        else:
            lax.fori_loop(start, stop, step, 0)
        for i in range(start, stop):
            sends.append(piece(i))

    def b_groups(a_all, count, arrived):
        def group(g, carry):
            @pl.when(g == 1)
            def _():
                arrived()
            b_rows(a_all, [jnp.where(g == 0, mine[i], theirs[i]) for i in range(count)])
            return carry
        lax.fori_loop(0, 2, group, 0)

    acc_ref[...] = jnp.zeros_like(acc_ref)
    share(a1_all, "a1", 0, 2)
    for k, piece in enumerate(c2_pieces(far, far_partner, core)):
        forward(piece, ("c2", k))
    for k, piece in enumerate(c2_pieces(far_partner, far, 1 - core)):
        partner_arrived(piece, ("far c2", k))
    first = (1 - chip) * 2 * MB
    second = first + MB
    for base in (first, second):
        mirror(c2_all, base, base + 128, c2_all, base + 128, base, 128)
    mirror(c2_all, second + 128, first, c2_all, first, second + 128, 128)
    mirror(c2_all, second + 128, first + 128, c2_all, first + 128, second + 128, 128)
    mirror(c2_all, first, second, c2_all, second, first, 128)
    mirror(c2_all, first + 128, second, c2_all, second, first + 128, 128)

    def a1_arrived():
        for i in range(2):
            partner_arrived(a_slice(a1_all, theirs[i]), ("a1", i))
    b_groups(a1_all, 2, a1_arrived)
    for k, piece in enumerate(c1_quads(NB, far_partner, core)):
        far_arrived(piece, ("c1 quad", k))
        go(to_partner(piece, quad_side.at[k * HALF:(k + 1) * HALF, :], ("c1 quad", k)))
    for k in range(2):
        partner_arrived(quad_side.at[k * HALF:(k + 1) * HALF, :], ("c1 quad", k))
    mirror(quad_side, 0, 0, c1_rows, NB, far_partner * NB + HALF, HALF)
    mirror(quad_side, HALF, 0, c1_rows, NB + (1 - core) * HALF, far_partner * NB + (1 - core) * HALF, HALF)

    def a_early(i, carry):
        rows = span(NB + i * CH, CH)
        for n in range(4):
            cols = slice(n * 256, (n + 1) * 256)
            kern[span(far * NB + i * CH, CH), cols] = (
                jnp.dot(c1_rows[rows, span(chip * 2 * NB, 2 * NB)], t_all[span(chip * 2 * NB, 2 * NB), cols],
                        preferred_element_type=F32)
                + jnp.dot(c1_rows[rows, span(far_partner * NB, NB)], t_all[span(far_partner * NB, NB), cols],
                          preferred_element_type=F32))
        return carry
    lax.fori_loop(0, 2, a_early, 0)

    def a_late(i):
        base = mine[2 + i]
        for n in range(4):
            cols = slice(n * 256, (n + 1) * 256)
            a1_all[span(base, CH), cols] = (
                kern[span(base, CH), cols]
                + jnp.dot(c1_rows[NB + i * CH:NB + (i + 1) * CH, span(far * NB, NB)], t_all[span(far * NB, NB), cols],
                          preferred_element_type=F32)).astype(BF16)
        go(to_partner(a_slice(a1_all, base), a_slice(a1_all, base), ("a1", 2 + i)))

    for i in range(2):
        for k in (2 * i, 2 * i + 1):
            far_arrived(c1_strip(NB, far, k), ("c1 strip", k))
            for below in range(k + 1, 4):
                mirror(c1_rows, NB + k * 128, far * NB + below * 128, c1_rows, NB + below * 128, far * NB + k * 128, 128)
        a_late(i)
        products(a1_all, mine[2 + i])
    for i in range(2):
        partner_arrived(a_slice(a1_all, theirs[2 + i]), ("a1", 2 + i))
        products(a1_all, theirs[2 + i])
    for half in range(2):
        forward(x_half(far, half), ("x", half))
        late_scores(mine[2 + half], raw0)
        form(mine[2 + half], raw0)
        partner_arrived(x_half(far_partner, half), ("far x", half))
        late_scores(theirs[2 + half], raw1)
        form(theirs[2 + half], raw1)
    store_col_scale([acc_ref[:, col(j)] for j in range(COLS)], v_ref, q_ref)
    sweeps(SWEEPS - 1, kern, p_b, u_b, v_ref, q_ref, 32)

    for copy in sends:
        copy.wait_send()
    sends.clear()

    def next_plan(i, carry):
        row = hint(i * 64, 64)
        for j, t in scaled_rows(kern, u_b, v_ref, row, 64):
            t_all[pl.ds(row, 64), col(j)] = t.astype(BF16)
        return carry
    lax.fori_loop(0, N // 64, next_plan, 0)

    acc_ref[...] = jnp.zeros_like(acc_ref)
    first_slot = SIDE.names[("a2", 0)]

    def a2_piece(i):
        ref = a2_all.at[span(jnp.where(i == 0, me, far) * NB, NB), :]
        return pltpu.make_async_remote_copy(
            src_ref=ref, dst_ref=ref, send_sem=side_send.at[first_slot + i], recv_sem=side_recv.at[first_slot + i],
            device_id={"rows": partner}, device_id_type=pl.DeviceIdType.MESH)

    def a2_step(i, carry):
        a_rows(a2_all, i * NB, jnp.where(i == 0, me, far) * NB, NB)
        a2_piece(i).start()
        return carry
    lax.fori_loop(0, 2, a2_step, 0)
    sends.extend((a2_piece(0), a2_piece(1)))

    def a2_arrived():
        for i in range(2):
            a2_piece(i).wait_recv()
    b_groups(a2_all, 4, a2_arrived)
    store_col_scale([acc_ref[:, col(j)] for j in range(COLS)], v_ref, q_ref)
    sweeps(SWEEPS - 1, kern, p_b, u_b, v_ref, q_ref, 16)


    def result(i, carry):
        row = hint(i * 64, 64)
        for j, t in scaled_rows(kern, u_b, v_ref, hint(me * NB + row, 64), 64):
            out_ref[pl.ds(row, 64), col(j)] = t
        return carry
    lax.fori_loop(0, NB // 64, result, 0)
    for copy in sends:
        copy.wait_send()


def solution(mesh):
    vmem = pl.BlockSpec(memory_space=pltpu.VMEM)
    hbm = pl.BlockSpec(memory_space=pl.ANY)
    smem = pl.BlockSpec(memory_space=pltpu.SMEM)

    def local_fgw(cost_src, cost_tgt, plan_init, mass_src, mass_tgt, feat_src, feat_tgt, epsilon):
        return pl.pallas_call(
            kernel,
            out_shape=pltpu.VMEM((NB, M), F32),
            in_specs=[hbm] * 7 + [smem],
            out_specs=vmem,
            scratch_shapes=[
                pltpu.VMEM((1, M), F32),
                pltpu.VMEM((NB, M), F32),
                pltpu.VMEM((N, M), BF16),
                pltpu.VMEM((2 * NB, N), BF16),
                pltpu.VMEM((NB, NB), BF16),
                pltpu.VMEM((2 * HALF, HALF), BF16),
                pltpu.VMEM((M, M), BF16),
                pltpu.VMEM((M, D), BF16),
                pltpu.VMEM((N, D), BF16),
                pltpu.VMEM((N, M), F32),
                pltpu.VMEM((N, M), BF16),
                pltpu.VMEM((N, M), BF16),
                pltpu.VMEM((N, M), F32),
                pltpu.VMEM((4, NB // LANES, LANES), F32),
                pltpu.VMEM((N, LANES), F32),
                pltpu.VMEM((N, LANES), F32),
                pltpu.VMEM((2 * CH, LANES), F32),
                pltpu.VMEM((2 * CH, LANES), F32),
                pltpu.VMEM((8, M), F32),
                pltpu.VMEM((8, M), F32),
                pltpu.SemaphoreType.DMA((8,)),
                pltpu.SemaphoreType.DMA((len(LINK.names),)),
                pltpu.SemaphoreType.DMA((len(LINK.names),)),
                pltpu.SemaphoreType.DMA((len(SIDE.names),)),
                pltpu.SemaphoreType.DMA((len(SIDE.names),)),
            ],
            compiler_params=pltpu.CompilerParams(
                collective_id=0, has_side_effects=True, vmem_limit_bytes=54000 * 1024),
        )(*(pltpu.with_memory_space_constraint(x, pltpu.HBM) for x in (
            cost_src, cost_tgt, plan_init, mass_src.reshape(NB // LANES, LANES), mass_tgt.reshape(1, M),
            feat_src, feat_tgt)), epsilon.reshape(1, 1))

    row_spec = P(('pairs', 'rows'), None)
    vec_spec = P(('pairs', 'rows'))
    in_specs = (row_spec, row_spec, row_spec, vec_spec, P('pairs'), row_spec, row_spec, P())
    return jax.shard_map(local_fgw, mesh=mesh, in_specs=in_specs, out_specs=row_spec, check_vma=False)
```

profile of v0, /device:TPU:0, one launch (start us, length us, event | category | flops | bytes accessed | tf_op | source)
XLA Modules:
  0.0 90.1 jit_solution(5853105896958888562)
XLA Ops:
  0.7 88.1 %shard_map.82 = f32[512,1024]{1,0:T(8,128)S(1)} custom-call(f32[512,2048]{1,0:T(8,128)} %c1_hbm.1, f32[256,1024]{1,0:T(8,128)} %c2_hbm.1, f32[512,1024]{1,0:T(8,128)} %t0_hbm.1, f32[4,128]{1,0:T(4,128)} %bitcast.5, f32[1,1024]{1,0:T(1,128)} %bitcast.4, f32[512,256]{1,0:T(8,128)} %x_hbm.1, f32[256,256]{1,0:T(8,128)} %y_hbm.1, f32[1,1]{1,0:T(1,128)} %bitcast.3.eps_ref), custom_call_target="tpu_custom_call" | custom-call | tf_op jit(solution)/shard_map/pallas_call | solution.py:494
  88.8 1.3 %copy.10 = f32[512,1024]{1,0:T(8,128)} copy(f32[512,1024]{1,0:T(8,128)S(1)} %shard_map.82) | data formatting | bytes 4194304
where the time goes:
time: 90.2 us; the launch traced here: 90.1 us
  Pallas kernels  88.1 us (98%)
  local copies, waits for them, and re-layouts  1.32 us (1%)
    pallas_call x1, Pallas kernels, local_fgw(): pl.pallas_call(kernel, out_shape=pltpu.VMEM((NB, M), F32), in_specs=[hbm]...  88.1 us

commit v1 on v0

--- a/solution.py
+++ b/solution.py
@@ -20,7 +20,7 @@
 LANES = 128
 COLS = M // LANES
 
-T_CHUNKS = 4
+T_CHUNKS = 2
 TR = NB // T_CHUNKS
 CH = 256
 HALF = NB // 2
@@ -325,9 +325,9 @@
         for i, base in enumerate(bases):
             if ready and ready[i]:
                 ready[i]()
-            scores(a_all, base, raws[i % 2])
             if i:
                 form(bases[i - 1], raws[(i - 1) % 2])
+            scores(a_all, base, raws[i % 2])
         form(bases[-1], raws[(len(bases) - 1) % 2])
 
     def a_slice(a_all, base):
@@ -445,11 +445,11 @@
     sends.clear()
 
     def next_plan(i, carry):
-        row = hint(i * 64, 64)
-        for j, t in scaled_rows(kern, u_b, v_ref, row, 64):
-            t_all[pl.ds(row, 64), col(j)] = t.astype(BF16)
+        row = hint(i * 128, 128)
+        for j, t in scaled_rows(kern, u_b, v_ref, row, 128):
+            t_all[pl.ds(row, 128), col(j)] = t.astype(BF16)
         return carry
-    lax.fori_loop(0, N // 64, next_plan, 0)
+    lax.fori_loop(0, N // 128, next_plan, 0)
 
     acc_ref[...] = jnp.zeros_like(acc_ref)
     first_slot = SIDE.names[("a2", 0)]

time: 90.2 us -> 90.3 us (level)
  no operation moved by 1% of the time
where the time goes in v1:
time: 90.3 us; the launch traced here: 90.2 us
  Pallas kernels  88.2 us (98%)
  local copies, waits for them, and re-layouts  1.32 us (1%)
    pallas_call x1, Pallas kernels, local_fgw(): pl.pallas_call(kernel, out_shape=pltpu.VMEM((NB, M), F32), in_specs=[hbm]...  88.2 us

profile of v1, /device:TPU:0, one launch (start us, length us, event | category | flops | bytes accessed | tf_op | source)
XLA Modules:
  0.0 90.2 jit_solution(12308808921859897020)
XLA Ops:
  0.7 88.2 %shard_map.82 = f32[512,1024]{1,0:T(8,128)S(1)} custom-call(f32[512,2048]{1,0:T(8,128)} %c1_hbm.1, f32[256,1024]{1,0:T(8,128)} %c2_hbm.1, f32[512,1024]{1,0:T(8,128)} %t0_hbm.1, f32[4,128]{1,0:T(4,128)} %bitcast.5, f32[1,1024]{1,0:T(1,128)} %bitcast.4, f32[512,256]{1,0:T(8,128)} %x_hbm.1, f32[256,256]{1,0:T(8,128)} %y_hbm.1, f32[1,1]{1,0:T(1,128)} %bitcast.3.eps_ref), custom_call_target="tpu_custom_call" | custom-call | tf_op jit(solution)/shard_map/pallas_call | solution.py:494
  88.9 1.3 %copy.10 = f32[512,1024]{1,0:T(8,128)} copy(f32[512,1024]{1,0:T(8,128)S(1)} %shard_map.82) | data formatting | bytes 4194304
